TPU v7x, 32 devices: a whole 2x2x4 slice. The times are simulated.
32 devices in a mesh: bank: 4 (over y, core), zero: 8 (over z, x).
Axes of the slice: x: 2, y: 2, z: 4, core: 2. Of those that a mesh axis runs over, the one named last changes fastest.
Arguments:
- train_gate: float32 [128, 2048, 768], P('bank', 'zero'), may hold values from -0.1875 to 0.1875
- other_gate: bfloat16 [128, 2048, 768], P('bank', 'zero'), may hold values from -0.0625 to 0.0625
- train_up: float32 [128, 2048, 768], P('bank', 'zero'), may hold values from -0.1875 to 0.1875
- other_up: bfloat16 [128, 2048, 768], P('bank', 'zero'), may hold values from -0.0625 to 0.0625
- router_weight: float32 [2048, 128], P('zero', 'bank'), may hold values from -0.125 to 0.125
- router_gain: float32 [2048], P('zero'), may hold values from 0.25 to 1.75
Outputs:
- ready_gate: bfloat16 [128, 2048, 768], P(('bank', 'zero'))
- ready_up: bfloat16 [128, 2048, 768], P(('bank', 'zero'))
- scale_gate: float32 [128, 768], P(('bank', 'zero'))
- scale_up: float32 [128, 768], P(('bank', 'zero'))
- serve_router: bfloat16 [2048, 128], replicated
All inputs are finite; a program needn't handle non-finite values.
Results may differ from a plain program's by a relative error of at most 0.0075.
Values may be sent and summed in bfloat16 or wider, within the bound.
A program may use at most 192 MiB of HBM per device.

v0:
```python
import jax
import jax.numpy as jnp
from jax import lax
from jax.sharding import PartitionSpec as P


def body(train_gate, other_gate, train_up, other_up, router_weight, router_gain):
    latest_gate = train_gate + other_gate.astype(jnp.float32)
    latest_up = train_up + other_up.astype(jnp.float32)
    total_gate, total_up = (
        lax.psum(jnp.sum(latest_gate * latest_gate, axis=1).astype(jnp.bfloat16), "zero").astype(
            jnp.float32
        ),
        lax.psum(jnp.sum(latest_up * latest_up, axis=1).astype(jnp.bfloat16), "zero").astype(
            jnp.float32
        ),
    )
    scale_gate = jnp.sqrt(total_gate)
    scale_up = jnp.sqrt(total_up)
    narrow_gate, narrow_up = (
        (latest_gate / jnp.expand_dims(scale_gate, 1)).astype(jnp.bfloat16),
        (latest_up / jnp.expand_dims(scale_up, 1)).astype(jnp.bfloat16),
    )
    ready_gate, ready_up = (
        lax.all_to_all(narrow_gate, "zero", split_axis=0, concat_axis=1, tiled=True),
        lax.all_to_all(narrow_up, "zero", split_axis=0, concat_axis=1, tiled=True),
    )
    scale_gate = lax.dynamic_slice_in_dim(
        scale_gate, lax.axis_index("zero") * ready_gate.shape[0], ready_gate.shape[0], axis=0
    )
    scale_up = lax.dynamic_slice_in_dim(
        scale_up, lax.axis_index("zero") * ready_up.shape[0], ready_up.shape[0], axis=0
    )
    part_router = (router_weight * router_gain[:, None]).astype(jnp.bfloat16)
    row_router = lax.all_gather(part_router, "zero", axis=0, tiled=True)
    serve_router = lax.all_gather(row_router, "bank", axis=1, tiled=True)
    return (ready_gate, ready_up, scale_gate, scale_up, serve_router)


def solution(mesh):
    placed = (
        P("bank", "zero", None),
        P("bank", "zero", None),
        P("bank", "zero", None),
        P("bank", "zero", None),
        P("zero", "bank"),
        P("zero"),
    )
    return jax.shard_map(
        body,
        mesh=mesh,
        in_specs=placed,
        out_specs=(
            P(("bank", "zero"), None, None),
            P(("bank", "zero"), None, None),
            P(("bank", "zero"), None),
            P(("bank", "zero"), None),
            P(),
        ),
        check_vma=False,
    )
```

profile of v0, /device:TPU:0, one launch (start us, length us, event | category | flops | bytes accessed | tf_op | source)
XLA Modules:
  0.0 735.0 jit_solution(10002931296781212974)
XLA Ops:
  7.2 0.0 all-reduce.3.cloned.1.call-start
  7.2 25.1 %multiply_reduce_fusion = (bf16[32,768]{1,0:T(8,128)(2,1)}, bf16[32,768]{1,0:T(8,128)(2,1)}) fusion(f32[32,256,768]{2,1,0:T(8,128)} %param.8, bf16[32,256,768]{2,1,0:T(8,128)(2,1)} %param.9, f32[32,256,768]{2,1,0:T(8,128)} %param.6, bf16[32,256,768]{2,1,0:T(8,128)(2,1)} %param.7), kind=kLoop, calls=%fused_computation.1 | loop fusion | flops 50282496 | bytes 75595776 | tf_op jit(solution)/shard_map/reduce_sum | solution.py:14
  32.4 0.0 all-reduce.3.cloned.1.call-update
  32.4 73.3 %all-reduce.3.cloned.1.call-done = (bf16[32,768]{1,0:T(8,128)(2,1)}, bf16[32,768]{1,0:T(8,128)(2,1)}) async-done(((bf16[32,768]{1,0:T(8,128)(2,1)}, bf16[32,768]{1,0:T(8,128)(2,1)}), (bf16[32,768]{1,0:T(8,128)(2,1)}, bf16[32,768]{1,0:T(8,128)(2,1)})) %all-reduce.3.cloned.1.call-update) | async-done | bytes 98320 | tf_op jit(solution)/shard_map/psum | solution.py:11
  105.7 0.8 convert_sqrt_fusion.1
  106.6 17.2 %divide_convert_fusion.1 = bf16[32,256,768]{2,1,0:T(8,128)(2,1)} fusion(f32[32,256,768]{2,1,0:T(8,128)} %param.6, bf16[32,256,768]{2,1,0:T(8,128)(2,1)} %param.7, f32[32,768]{1,0:T(8,128)S(1)} %convert_sqrt_fusion.1), kind=kLoop, calls=%fused_computation.3 | loop fusion | flops 25165824 | bytes 50429952 | tf_op jit(solution)/shard_map/convert_element_type | solution.py:21
  123.8 0.0 copy-start
  123.8 5.5 all-to-all-start
  129.3 0.0 copy-done
  129.3 17.4 %divide_convert_fusion = bf16[32,256,768]{2,1,0:T(8,128)(2,1)} fusion(f32[32,256,768]{2,1,0:T(8,128)} %param.8, bf16[32,256,768]{2,1,0:T(8,128)(2,1)} %param.9, f32[32,768]{1,0:T(8,128)S(1)} %convert_sqrt_fusion), kind=kLoop, calls=%fused_computation | loop fusion | flops 25165824 | bytes 50429952 | tf_op jit(solution)/shard_map/convert_element_type | solution.py:22
  146.7 0.0 copy-start.1
  146.7 0.0 copy-start.2
  146.7 253.8 %all-to-all-done = bf16[32,256,768]{2,1,0:T(8,128)(2,1)} async-done(((bf16[32,256,768]{2,1,0:T(8,128)(2,1)}), bf16[32,256,768]{2,1,0:T(8,128)(2,1)}, u32[]{:S(2)}, u32[]{:S(2)}) %all-to-all-start) | async-done | bytes 12582944 | tf_op jit(solution)/shard_map/all_to_all | solution.py:25
  400.5 5.4 all-to-all-start.1
  405.9 0.0 copy-done.1
  405.9 0.0 copy-done.2
  405.9 291.6 %all_gather.6 = bf16[2048,32]{0,1:T(8,128)(2,1)S(1)} all-gather(bf16[256,32]{0,1:T(8,128)(2,1)S(1)} %multiply_convert_fusion), channel_id=1, replica_groups=mesh['bank'=4,'zero'=8] {'zero'}, dimensions={0}, use_global_device_ids=true | all-gather | bytes 147456 | tf_op jit(solution)/shard_map/all_gather | solution.py:35
  697.5 7.1 all_gather.7
  704.6 1.0 copy.16
  705.6 0.6 constant_dynamic-slice_fusion
  706.2 0.6 constant_dynamic-slice_fusion.1
  706.8 10.7 %copy.14 = bf16[8,4,256,768]{3,2,0,1:T(8,128)(2,1)} copy(bf16[8,4,256,768]{3,2,1,0:T(8,128)(2,1)} %bitcast) | data formatting | bytes 25165824 | tf_op jit(solution)/shard_map/all_to_all | solution.py:25
  717.5 0.0 all-to-all-done.1
  717.5 10.7 %copy.15 = bf16[8,4,256,768]{3,2,0,1:T(8,128)(2,1)} copy(bf16[8,4,256,768]{3,2,1,0:T(8,128)(2,1)} %bitcast.3) | data formatting | bytes 25165824 | tf_op jit(solution)/shard_map/all_to_all | solution.py:26
  (2 shorter events, 0.0 us)
Async XLA Ops:
  7.2 98.6 %all-reduce.3.cloned.1.call-start = ((), (), s32[]{:S(2)}) async-start(), calls=%async_computation.2 | async-start | bytes 196608 | tf_op jit(solution)/shard_map/psum | solution.py:11
  123.8 5.5 copy-start
  123.8 276.7 %all-to-all-start = ((bf16[32,256,768]{2,1,0:T(8,128)(2,1)}), bf16[32,256,768]{2,1,0:T(8,128)(2,1)}, u32[]{:S(2)}, u32[]{:S(2)}) async-start(bf16[32,256,768]{2,1,0:T(8,128)(2,1)} %divide_convert_fusion.1), calls=%async_computation | async-start | bytes 25165824 | tf_op jit(solution)/shard_map/all_to_all | solution.py:25
  146.7 259.2 %copy-start.1 = (f32[256,32]{0,1:T(8,128)S(1)}, f32[256,32]{0,1:T(8,128)}, u32[]{:S(2)}) copy-start(f32[256,32]{0,1:T(8,128)} %param.10) | copy-start | bytes 98308
  146.7 259.2 %copy-start.2 = (f32[256]{0:T(256)S(1)}, f32[256]{0:T(256)}, u32[]{:S(2)}) copy-start(f32[256]{0:T(256)} %param.11) | copy-start | bytes 3076
  400.5 317.0 %all-to-all-start.1 = ((bf16[32,256,768]{2,1,0:T(8,128)(2,1)}), bf16[32,256,768]{2,1,0:T(8,128)(2,1)}, u32[]{:S(2)}, u32[]{:S(2)}) async-start(bf16[32,256,768]{2,1,0:T(8,128)(2,1)} %divide_convert_fusion), calls=%async_computation.1 | async-start | bytes 25165824 | tf_op jit(solution)/shard_map/all_to_all | solution.py:26
Sparse Core Ops, SparseCore 0:
  32.5 73.1 all-reduce.2
where the time goes:
time: 735 us
  waiting for transfers between devices  327 us (44%)
  blocking collectives  299 us (41%)
  other arithmetic  60.6 us (8%)
  local copies, waits for them, and re-layouts  23.6 us (3%)
  between operations  14.1 us (2%)
  starting transfers between devices  10.9 us (1%)
    all_gather x1, blocking collectives, body(): row_router = lax.all_gather(part_router, 'zero', axis=0, tiled=True)  292 us
    all_to_all x1, waiting for transfers between devices, body(): lax.all_to_all(narrow_gate, 'zero', split_axis=0, concat_axis=1, tiled=True)  254 us
    psum x1, waiting for transfers between devices, body(): lax.psum(jnp.sum(latest_gate * latest_gate, axis=1).astype(jnp.bfloat16),...  73.3 us
    reduce_sum x1, other arithmetic, body(): jnp.sum(latest_up * latest_up, axis=1).astype(jnp.bfloat16)  25.1 us
    convert_element_type x1, other arithmetic, body(): (latest_up / jnp.expand_dims(scale_up, 1)).astype(jnp.bfloat16)  17.4 us
    convert_element_type x1, other arithmetic, body(): (latest_gate / jnp.expand_dims(scale_gate, 1)).astype(jnp.bfloat16)  17.2 us
  transfers between devices with their start and end apart: 3, of which 2 were waited for; matrix products, arithmetic and copies ran while one was open for 4% of the time, Pallas kernels for 0%

commit v1 on v0

--- a/solution.py
+++ b/solution.py
@@ -4,13 +4,18 @@
 from jax.sharding import PartitionSpec as P
 
 
+def gather_and_add(x, mesh_axis):
+    pieces = lax.all_gather(x, mesh_axis)
+    return jnp.sum(pieces, axis=0)
+
+
 def body(train_gate, other_gate, train_up, other_up, router_weight, router_gain):
     latest_gate = train_gate + other_gate.astype(jnp.float32)
     latest_up = train_up + other_up.astype(jnp.float32)
     total_gate, total_up = (
-        lax.psum(jnp.sum(latest_gate * latest_gate, axis=1).astype(jnp.bfloat16), "zero").astype(
-            jnp.float32
-        ),
+        gather_and_add(
+            jnp.sum(latest_gate * latest_gate, axis=1).astype(jnp.bfloat16), "zero"
+        ).astype(jnp.float32),
         lax.psum(jnp.sum(latest_up * latest_up, axis=1).astype(jnp.bfloat16), "zero").astype(
             jnp.float32
         ),

time: 735 us -> 700 us (0.952)
  waiting for transfers between devices: 327 us -> 0.01 us
  blocking collectives: 299 us -> 604 us
  between operations: 14.1 us -> 0.71 us
    psum x0 -> x1, blocking collectives: none -> 278 us  [body(): lax.psum(jnp.sum(latest_up * latest_up, axis=1).astype(jnp.bfloat16), 'ze...]
    all_to_all x1, waiting for transfers between devices: 254 us -> 0.01 us  [body(): lax.all_to_all(narrow_gate, 'zero', split_axis=0, concat_axis=1, tiled=True)]
    psum x1 -> x0, waiting for transfers between devices: 73.3 us -> none  [body(): lax.psum(jnp.sum(latest_gate * latest_gate, axis=1).astype(jnp.bfloat16),...]
    all_gather x0 -> x1, blocking collectives: none -> 32.8 us  [gather_and_add(): pieces = lax.all_gather(x, mesh_axis)]
    reduce_sum x0 -> x2, other arithmetic: none -> 12.9 us  [the longest x1 12.8 us: body(): jnp.sum(latest_gate * latest_gate, axis=1).astype(jnp.bfloat16)]
    reduce_sum x1, other arithmetic: 25.1 us -> 12.8 us  [body(): jnp.sum(latest_up * latest_up, axis=1).astype(jnp.bfloat16)]
  transfers between devices with their start and end apart: 3 -> 2, of which waited for: 2 -> 0; matrix products, arithmetic and copies ran while one was open for 4% -> 6% of each run, Pallas kernels for 0% -> 0%
where the time goes in v1:
time: 700 us
  blocking collectives  604 us (86%)
  other arithmetic  60.5 us (9%)
  local copies, waits for them, and re-layouts  23.6 us (3%)
  starting transfers between devices  11.1 us (2%)
    all_gather x1, blocking collectives, body(): row_router = lax.all_gather(part_router, 'zero', axis=0, tiled=True)  286 us
    psum x1, blocking collectives, body(): lax.psum(jnp.sum(latest_up * latest_up, axis=1).astype(jnp.bfloat16), 'ze...  278 us
    all_gather x1, blocking collectives, gather_and_add(): pieces = lax.all_gather(x, mesh_axis)  32.8 us
    convert_element_type x1, other arithmetic, body(): (latest_up / jnp.expand_dims(scale_up, 1)).astype(jnp.bfloat16)  17.4 us
    convert_element_type x1, other arithmetic, body(): (latest_gate / jnp.expand_dims(scale_gate, 1)).astype(jnp.bfloat16)  17.2 us
  transfers between devices with their start and end apart: 2, of which 0 were waited for; matrix products, arithmetic and copies ran while one was open for 6% of the time, Pallas kernels for 0%

profile of v1, /device:TPU:0, one launch (start us, length us, event | category | flops | bytes accessed | tf_op | source)
XLA Modules:
  0.0 699.6 jit_solution(13801321754549594710)
XLA Ops:
  0.6 12.8 %multiply_reduce_fusion.1 = bf16[32,768]{1,0:T(8,128)(2,1)S(1)} fusion(f32[32,256,768]{2,1,0:T(8,128)} %param.6, bf16[32,256,768]{2,1,0:T(8,128)(2,1)} %param.7), kind=kLoop, calls=%fused_computation.4 | loop fusion | flops 25141248 | bytes 37797888 | tf_op jit(solution)/shard_map/reduce_sum | solution.py:17
  13.5 32.8 %all-gather = bf16[256,768]{1,0:T(8,128)(2,1)S(1)} all-gather(bf16[32,768]{1,0:T(8,128)(2,1)S(1)} %multiply_reduce_fusion.1), channel_id=2, replica_groups=mesh['bank'=4,'zero'=8] {'zero'}, dimensions={0}, use_global_device_ids=true | all-gather | bytes 442368 | tf_op jit(solution)/shard_map/all_gather | solution.py:8
  46.3 0.1 reduce_sum.31
  46.4 17.2 %divide_convert_fusion.1 = bf16[32,256,768]{2,1,0:T(8,128)(2,1)} fusion(f32[32,256,768]{2,1,0:T(8,128)} %param.6, bf16[32,256,768]{2,1,0:T(8,128)(2,1)} %param.7, f32[32,768]{1,0:T(8,128)S(1)} %convert_sqrt_fusion.1), kind=kLoop, calls=%fused_computation.3 | loop fusion | flops 25165824 | bytes 50429952 | tf_op jit(solution)/shard_map/convert_element_type | solution.py:26
  63.6 5.6 all-to-all-start
  69.2 12.8 %multiply_reduce_fusion = bf16[32,768]{1,0:T(8,128)(2,1)S(1)} fusion(f32[32,256,768]{2,1,0:T(8,128)} %param.8, bf16[32,256,768]{2,1,0:T(8,128)(2,1)} %param.9), kind=kLoop, calls=%fused_computation.1 | loop fusion | flops 25141248 | bytes 37797888 | tf_op jit(solution)/shard_map/reduce_sum | solution.py:19
  82.0 277.7 %psum.7 = bf16[32,768]{1,0:T(8,128)(2,1)S(1)} all-reduce(bf16[32,768]{1,0:T(8,128)(2,1)S(1)} %multiply_reduce_fusion), channel_id=1, replica_groups=mesh['bank'=4,'zero'=8] {'zero'}, use_global_device_ids=true, to_apply=%region_3.0 | all-reduce | flops 24576 | bytes 98304 | tf_op jit(solution)/shard_map/psum | solution.py:19
  359.8 17.4 %divide_convert_fusion = bf16[32,256,768]{2,1,0:T(8,128)(2,1)} fusion(f32[32,256,768]{2,1,0:T(8,128)} %param.8, bf16[32,256,768]{2,1,0:T(8,128)(2,1)} %param.9, f32[32,768]{1,0:T(8,128)S(1)} %convert_sqrt_fusion), kind=kLoop, calls=%fused_computation | loop fusion | flops 25165824 | bytes 50429952 | tf_op jit(solution)/shard_map/convert_element_type | solution.py:27
  377.2 0.0 copy-start
  377.2 0.0 copy-start.1
  377.2 0.0 all-to-all-done
  377.2 5.5 all-to-all-start.1
  382.7 0.0 copy-done
  382.8 0.0 copy-done.1
  382.8 286.1 %all_gather.11 = bf16[2048,32]{0,1:T(8,128)(2,1)S(1)} all-gather(bf16[256,32]{0,1:T(8,128)(2,1)S(1)} %multiply_convert_fusion), channel_id=1, replica_groups=mesh['bank'=4,'zero'=8] {'zero'}, dimensions={0}, use_global_device_ids=true | all-gather | bytes 147456 | tf_op jit(solution)/shard_map/all_gather | solution.py:40
  668.9 7.2 %all_gather.12 = bf16[2048,128]{0,1:T(8,128)(2,1)S(1)} all-gather(bf16[2048,32]{0,1:T(8,128)(2,1)S(1)} %all_gather.11), channel_id=1, replica_groups=mesh['bank'=4,'zero'=8] {'bank'}, dimensions={1}, use_global_device_ids=true | all-gather | bytes 655360 | tf_op jit(solution)/shard_map/all_gather | solution.py:41
  676.0 1.0 copy.19
  677.0 0.6 constant_dynamic-slice_fusion.1
  677.7 0.6 constant_dynamic-slice_fusion
  678.3 10.7 %copy.17 = bf16[8,4,256,768]{3,2,0,1:T(8,128)(2,1)} copy(bf16[8,4,256,768]{3,2,1,0:T(8,128)(2,1)} %bitcast.1) | data formatting | bytes 25165824 | tf_op jit(solution)/shard_map/all_to_all | solution.py:30
  688.9 0.0 all-to-all-done.1
  688.9 10.7 %copy.18 = bf16[8,4,256,768]{3,2,0,1:T(8,128)(2,1)} copy(bf16[8,4,256,768]{3,2,1,0:T(8,128)(2,1)} %bitcast.4) | data formatting | bytes 25165824 | tf_op jit(solution)/shard_map/all_to_all | solution.py:31
  (3 shorter events, 0.1 us)
Async XLA Ops:
  63.6 313.6 %all-to-all-start = ((bf16[32,256,768]{2,1,0:T(8,128)(2,1)}), bf16[32,256,768]{2,1,0:T(8,128)(2,1)}, u32[]{:S(2)}, u32[]{:S(2)}) async-start(bf16[32,256,768]{2,1,0:T(8,128)(2,1)} %divide_convert_fusion.1), calls=%async_computation | async-start | bytes 25165824 | tf_op jit(solution)/shard_map/all_to_all | solution.py:30
  377.2 5.6 copy-start
  377.2 5.6 copy-start.1
  377.2 311.7 %all-to-all-start.1 = ((bf16[32,256,768]{2,1,0:T(8,128)(2,1)}), bf16[32,256,768]{2,1,0:T(8,128)(2,1)}, u32[]{:S(2)}, u32[]{:S(2)}) async-start(bf16[32,256,768]{2,1,0:T(8,128)(2,1)} %divide_convert_fusion), calls=%async_computation.1 | async-start | bytes 25165824 | tf_op jit(solution)/shard_map/all_to_all | solution.py:31
